TPU v7x, 128 devices: a whole 4x4x4 slice. The times are simulated.
128 devices in a mesh: seq: 16 (over x_hi, z, core), tp: 8 (over y, x_lo).
Axes of the slice: x: 4 (x_hi: 2, x_lo: 2; x = x_hi * 2 + x_lo), y: 4, z: 4, core: 2. Of those that a mesh axis runs over, the one named last changes fastest.
Arguments:
- tokens: bfloat16 [2048, 8192], P('seq'), may hold values from -6 to 6
- conv_weight: float32 [4, 8192], replicated, may hold values from -3 to 3
- norm_gain: float32 [8192], replicated, may hold values from 0.25 to 1.75
- gate_weight: bfloat16 [8192, 14336], P('seq', 'tp'), may hold values from -0.0625 to 0.0625
- up_weight: bfloat16 [8192, 14336], P('seq', 'tp'), may hold values from -0.0625 to 0.0625
- down_weight: bfloat16 [14336, 8192], P('tp', 'seq'), may hold values from -0.046875 to 0.046875
Outputs:
- mixed_out: bfloat16 [2048, 8192], P(('seq', 'tp'))
All inputs are finite; a program needn't handle non-finite values.
Results may differ from a plain program's by a relative error of at most 0.03.
Values may be sent and summed in bfloat16 or wider, within the bound.
No kernel may reach another device: no remote copies, remote signals or barrier semaphores. Data moves between devices by JAX's collectives and lax.ppermute only.
A program may use at most 64 MiB of HBM per device.

v0:
```python
import jax
import jax.numpy as jnp
from jax import lax
from jax.sharding import PartitionSpec as P


def from_behind(shard, axis, by):
    peers = lax.axis_size(axis)
    pairs = [(i, i + by) for i in range(peers) if 0 <= i + by < peers]
    return lax.ppermute(shard, axis, pairs)


def split_up(shard, dim, peers):
    shape = shard.shape
    parts = shard.reshape(*shape[:dim], peers, shape[dim] // peers, *shape[dim + 1 :])
    return jnp.moveaxis(parts, dim, 0)


def summed_on_arrival(shard, axis, dim):
    parts = split_up(shard, dim, lax.axis_size(axis))
    arrived = lax.all_to_all(parts, axis, split_axis=0, concat_axis=0, tiled=True)
    return arrived.astype(jnp.float32).sum(axis=0)


def swiglu(both_sums, half_cols):
    return (jax.nn.silu(both_sums[:, :half_cols]) * both_sums[:, half_cols:]).astype(jnp.bfloat16)


def shards(tokens, conv_weight, norm_gain, gate_weight, up_weight, down_weight):
    tok_rows = tokens.shape[0]
    taps_count = conv_weight.shape[0]
    seq_count = lax.axis_size("seq")
    edge_rows = from_behind(tokens[tok_rows - (taps_count - 1) :], "seq", 1)
    extended = jnp.concatenate([edge_rows, tokens], 0).astype(jnp.float32)
    conv_out = jnp.zeros(tokens.shape, jnp.float32)
    for tap_index in range(taps_count):
        begin = taps_count - 1 - tap_index
        conv_out = conv_out + conv_weight[tap_index][None, :] * extended[begin : begin + tok_rows]
    scale_rms = lax.rsqrt(jnp.mean(conv_out * conv_out, axis=-1, keepdims=True) + 1e-05)
    normed = (conv_out * scale_rms * norm_gain[None, :]).astype(jnp.bfloat16)
    all_rows = lax.all_to_all(normed, "seq", split_axis=1, concat_axis=0, tiled=True)
    half_cols = gate_weight.shape[1]
    w_both = jnp.concatenate([gate_weight, up_weight], 1)
    gate_share = lax.psum_scatter(
        jnp.dot(all_rows, w_both, preferred_element_type=jnp.float32).astype(jnp.bfloat16),
        "seq",
        scatter_dimension=0,
        tiled=True,
    ).astype(jnp.float32)
    hidden = swiglu(gate_share, half_cols)
    out_terms = jnp.dot(
        lax.all_gather(hidden, "seq", axis=0, tiled=True),
        down_weight,
        preferred_element_type=jnp.float32,
    )
    col_width = out_terms.shape[1]
    out_terms = out_terms.reshape(seq_count, tok_rows, col_width)
    summed = summed_on_arrival(out_terms.astype(jnp.bfloat16), "tp", 1)
    rounded = summed.astype(jnp.bfloat16)
    mixed_out = lax.all_to_all(rounded, "seq", split_axis=0, concat_axis=2, tiled=True)
    return mixed_out.reshape(mixed_out.shape[1], mixed_out.shape[2])


def solution(mesh):
    in_specs = (P("seq", None), P(), P(), P("seq", "tp"), P("seq", "tp"), P("tp", "seq"))
    out_specs = P(("seq", "tp"), None)
    return jax.shard_map(shards, mesh=mesh, in_specs=in_specs, out_specs=out_specs, check_vma=False)
```

profile of v0, /device:TPU:1, one launch (start us, length us, event | category | flops | bytes accessed | tf_op | source)
XLA Modules:
  0.0 350.1 jit_solution(9454202880680602987)
XLA Ops:
  6.5 0.0 copy-start
  6.5 0.0 reduce-scatter.2.cloned.1.call-start
  6.5 1.1 slice.34
  7.6 4.9 %collective-permute-start = (bf16[3,8192]{1,0:T(4,128)(2,1)S(1)}, bf16[3,8192]{1,0:T(4,128)(2,1)S(1)}, u32[]{:S(2)}, u32[]{:S(2)}) collective-permute-start(bf16[3,8192]{1,0:T(4,128)(2,1)S(1)} %slice.34), channel_id=1, source_target_pairs={{0,8},{8,16},{16,24},{24,32},{32,40},{40,48},{48,56},{56,64},{64,7... | collective-permute-start | bytes 147464 | tf_op jit(solution)/shard_map/ppermute | solution.py:10
  12.5 1.4 fusion.9
  13.9 4.1 %copy.16 = bf16[128,8192]{0,1:T(8,128)(2,1)} copy(bf16[128,8192]{1,0:T(8,128)(2,1)} %param.6) | data formatting | bytes 4194304 | tf_op args[0]
  18.0 0.0 collective-permute-done
  18.0 1.8 copy.15
  19.8 3.7 %maximum_convert_fusion = f32[131,8192]{0,1:T(8,128)S(1)} fusion(bf16[128,8192]{0,1:T(8,128)(2,1)} %copy.16, bf16[3,8192]{0,1:T(8,128)(2,1)} %copy.15), kind=kLoop, calls=%fused_computation.8 | loop fusion | flops 4292608 | bytes 6438912 | tf_op jit(solution)/shard_map/convert_element_type | solution.py:34
  23.6 0.0 copy-start.1
  23.6 8.7 %multiply_reduce_fusion = (f32[128]{0:T(128)S(1)}, f32[128,8192]{0,1:T(8,128)S(1)}) fusion(f32[131,8192]{0,1:T(8,128)S(1)} %maximum_convert_fusion, f32[8192]{0:T(1024)S(1)} %bitcast.30, f32[8192]{0:T(1024)S(1)} %bitcast.31, f32[8192]{0:T(1024)S(1)} %bitcast.29, f32[8192]{0:T(1024)S(1)} %bitcast.28), kind=kLoop, calls=%fused_computation.10 | loop fusion | flops 9437056 | bytes 21103104 | tf_op jit(solution)/shard_map/reduce_sum | solution.py:39
  32.3 0.0 copy-done.1
  32.3 3.5 multiply_convert_fusion
  35.8 35.4 %all_to_all.39 = bf16[128,16,512]{0,2,1:T(8,128)(2,1)} all-to-all(bf16[128,16,512]{0,2,1:T(8,128)(2,1)S(1)} %bitcast.22), channel_id=1, replica_groups=mesh['seq'=16,'tp'=8] {'seq'}, dimensions={1} | all-to-all | bytes 4194304 | tf_op jit(solution)/shard_map/all_to_all | solution.py:41
  71.2 3.9 %copy.17 = bf16[16,128,512]{2,1,0:T(8,128)(2,1)} copy(bf16[16,128,512]{1,2,0:T(8,128)(2,1)} %bitcast.23) | data formatting | bytes 4194304 | tf_op jit(solution)/shard_map/all_to_all | solution.py:41
  75.1 13.4 %convolution_convert_fusion = bf16[2048,3584]{1,0:T(8,128)(2,1)} fusion(bf16[2048,512]{1,0:T(8,128)(2,1)} %bitcast.25, bf16[512,1792]{1,0:T(8,128)(2,1)} %param.10, bf16[512,1792]{1,0:T(8,128)(2,1)} %param.9), kind=kOutput, calls=%fused_computation | convolution fusion | flops 7530872832 | bytes 20447232 | tf_op jit(solution)/shard_map/dot_general | solution.py:45
  88.5 0.0 reduce-scatter.2.cloned.1.call-update
  88.5 0.0 all-gather.2.cloned.1.call-start
  88.6 129.9 %reduce-scatter.2.cloned.1.call-done = bf16[128,3584]{1,0:T(8,128)(2,1)} async-done(((bf16[2048,3584]{1,0:T(8,128)(2,1)}), bf16[128,3584]{1,0:T(8,128)(2,1)}) %reduce-scatter.2.cloned.1.call-update) | async-done | bytes 917520 | tf_op jit(solution)/shard_map/reduce_scatter | solution.py:44
  218.4 1.4 convert_element_type.27
  219.8 1.0 fusion.6
  220.8 0.0 all-gather.2.cloned.1.call-update
  220.8 67.8 %all-gather.2.cloned.1.call-done = bf16[2048,1792]{1,0:T(8,128)(2,1)} async-done(((bf16[128,1792]{1,0:T(8,128)(2,1)}), bf16[2048,1792]{1,0:T(8,128)(2,1)}) %all-gather.2.cloned.1.call-update) | async-done | bytes 7340048 | tf_op jit(solution)/shard_map/all_gather | solution.py:52
  288.6 0.0 copy-done
  288.7 7.3 %convolution_convert_fusion.1 = bf16[2048,512]{1,0:T(8,128)(2,1)S(1)} fusion(bf16[2048,1792]{1,0:T(8,128)(2,1)} %all-gather.2.cloned.1.call-done, bf16[1792,512]{1,0:T(8,128)(2,1)S(1)} %copy-done), kind=kOutput, calls=%fused_computation.14 | convolution fusion | flops 3759144960 | bytes 11272192 | tf_op jit(solution)/shard_map/dot_general | solution.py:51
  295.9 0.2 copy.25
  296.1 30.1 %all_to_all.40 = bf16[8,16,16,512]{3,2,1,0:T(8,128)(2,1)} all-to-all(bf16[8,16,16,512]{3,2,1,0:T(8,128)(2,1)S(1)} %bitcast.24), channel_id=1, replica_groups=mesh['seq'=16,'tp'=8] {'tp'}, dimensions={0} | all-to-all | bytes 4194304 | tf_op jit(solution)/shard_map/all_to_all | solution.py:21
  326.2 2.0 reduce_sum.22
  328.2 14.4 %all_to_all.41 = bf16[16,16,512]{2,1,0:T(8,128)(2,1)S(1)} all-to-all(bf16[16,16,512]{2,1,0:T(8,128)(2,1)S(1)} %reduce_sum.22), channel_id=1, replica_groups=mesh['seq'=16,'tp'=8] {'seq'}, dimensions={0} | all-to-all | bytes 524288 | tf_op jit(solution)/shard_map/all_to_all | solution.py:60
  342.6 0.7 copy.22
  (1 shorter events, 0.0 us)
Async XLA Ops:
  6.5 282.1 %copy-start = (bf16[1792,512]{1,0:T(8,128)(2,1)S(1)}, bf16[1792,512]{1,0:T(8,128)(2,1)}, u32[]{:S(2)}) copy-start(bf16[1792,512]{1,0:T(8,128)(2,1)} %param.11) | copy-start | bytes 5505028
  6.5 211.9 %reduce-scatter.2.cloned.1.call-start = ((), (), s32[]{:S(2)}) async-start(), calls=%async_computation.4 | async-start | bytes 15597568 | tf_op jit(solution)/shard_map/reduce_scatter | solution.py:44
  7.6 10.4 %collective-permute-start = (bf16[3,8192]{1,0:T(4,128)(2,1)S(1)}, bf16[3,8192]{1,0:T(4,128)(2,1)S(1)}, u32[]{:S(2)}, u32[]{:S(2)}) collective-permute-start(bf16[3,8192]{1,0:T(4,128)(2,1)S(1)} %slice.34), channel_id=1, source_target_pairs={{0,8},{8,16},{16,24},{24,32},{32,40},{40,48},{48,56},{56,64},{64,7... | collective-permute-start | bytes 147464 | tf_op jit(solution)/shard_map/ppermute | solution.py:10
  23.6 8.8 %copy-start.1 = (f32[8192]{0:T(1024)S(1)}, f32[8192]{0:T(1024)}, u32[]{:S(2)}) copy-start(f32[8192]{0:T(1024)} %param.8) | copy-start | bytes 98308
  88.5 200.1 %all-gather.2.cloned.1.call-start = ((), (), s32[]{:S(2)}) async-start(), calls=%async_computation.5 | async-start | bytes 7798784 | tf_op jit(solution)/shard_map/all_gather | solution.py:52
Sparse Core Ops, SparseCore 0:
  88.6 129.7 reduce-scatter.1
  221.0 67.6 all-gather.1
where the time goes:
time: 351 us; the launch traced here: 350 us
  waiting for transfers between devices  198 us (56%)
  blocking collectives  79.8 us (23%)
  matrix products  20.6 us (6%)
  other arithmetic  20.3 us (6%)
  between operations  13.5 us (4%)
  local copies, waits for them, and re-layouts  13.2 us (4%)
  starting transfers between devices  4.97 us (1%)
    reduce_scatter x1, waiting for transfers between devices, shards(): lax.psum_scatter(jnp.dot(all_rows, w_both, preferred_element_type=jnp.flo...  130 us
    all_gather x1, waiting for transfers between devices, shards(): lax.all_gather(hidden, 'seq', axis=0, tiled=True)  67.8 us
    all_to_all x1, blocking collectives, shards(): lax.all_to_all(normed, 'seq', split_axis=1, concat_axis=0, tiled=True)  35.4 us
    all_to_all x1, blocking collectives, summed_on_arrival(): lax.all_to_all(parts, axis, split_axis=0, concat_axis=0, tiled=True)  30.1 us
    all_to_all x1, blocking collectives, shards(): lax.all_to_all(rounded, 'seq', split_axis=0, concat_axis=2, tiled=True)  14.4 us
    dot_general x1, matrix products, shards(): jnp.dot(all_rows, w_both, preferred_element_type=jnp.float32)  13.4 us
    reduce_sum x1, other arithmetic, shards(): jnp.mean(conv_out * conv_out, axis=-1, keepdims=True) + 1e-05  8.75 us
    dot_general x1, matrix products, shards(): jnp.dot(lax.all_gather(hidden, 'seq', axis=0, tiled=True), down_weight, p...  7.26 us
  transfers between devices with their start and end apart: 3, of which 2 were waited for; matrix products, arithmetic and copies ran while one was open for 2% of the time, Pallas kernels for 0%

commit v1 on v0

--- a/solution.py
+++ b/solution.py
@@ -2,6 +2,13 @@
 import jax.numpy as jnp
 from jax import lax
 from jax.sharding import PartitionSpec as P
+
+
+def stacked_exchange(array, axis, split, join):
+    count = lax.axis_size(axis)
+    blocks = jnp.stack(jnp.split(array, count, axis=split), axis=0)
+    blocks = lax.all_to_all(blocks, axis, split_axis=0, concat_axis=0)
+    return jnp.concatenate(blocks, axis=join)
 
 
 def from_behind(shard, axis, by):
@@ -38,7 +45,7 @@
         conv_out = conv_out + conv_weight[tap_index][None, :] * extended[begin : begin + tok_rows]
     scale_rms = lax.rsqrt(jnp.mean(conv_out * conv_out, axis=-1, keepdims=True) + 1e-05)
     normed = (conv_out * scale_rms * norm_gain[None, :]).astype(jnp.bfloat16)
-    all_rows = lax.all_to_all(normed, "seq", split_axis=1, concat_axis=0, tiled=True)
+    all_rows = stacked_exchange(normed, "seq", 1, 0)
     half_cols = gate_weight.shape[1]
     w_both = jnp.concatenate([gate_weight, up_weight], 1)
     gate_share = lax.psum_scatter(

time: 351 us -> 329 us (0.937)
  other arithmetic: 20.3 us -> 9.25 us
  local copies, waits for them, and re-layouts: 13.2 us -> 3.46 us
    reduce_sum x1, other arithmetic: 8.75 us -> 2.21 us  [shards(): jnp.mean(conv_out * conv_out, axis=-1, keepdims=True) + 1e-05]
    all_to_all x1 -> x0, local copies, waits for them, and re-layouts: 3.93 us -> none  [shards(): lax.all_to_all(normed, 'seq', split_axis=1, concat_axis=0, tiled=True)]
    unnamed x6 -> x24, local copies, waits for them, and re-layouts: 4.82 us -> 0.91 us
  transfers between devices with their start and end apart: 3 -> 3, of which waited for: 2 -> 2; matrix products, arithmetic and copies ran while one was open for 2% -> 0% of each run, Pallas kernels for 0% -> 0%
where the time goes in v1:
time: 329 us
  waiting for transfers between devices  198 us (60%)
  blocking collectives  81.3 us (25%)
  matrix products  18.6 us (6%)
  between operations  13.6 us (4%)
  other arithmetic  9.25 us (3%)
  starting transfers between devices  4.97 us (2%)
  local copies, waits for them, and re-layouts  3.46 us (1%)
    reduce_scatter x1, waiting for transfers between devices, shards(): lax.psum_scatter(jnp.dot(all_rows, w_both, preferred_element_type=jnp.flo...  130 us
    all_gather x1, waiting for transfers between devices, shards(): lax.all_gather(hidden, 'seq', axis=0, tiled=True)  67.8 us
    all_to_all x1, blocking collectives, stacked_exchange(): blocks = lax.all_to_all(blocks, axis, split_axis=0, concat_axis=0)  36.8 us
    all_to_all x1, blocking collectives, summed_on_arrival(): lax.all_to_all(parts, axis, split_axis=0, concat_axis=0, tiled=True)  30.1 us
    all_to_all x1, blocking collectives, shards(): lax.all_to_all(rounded, 'seq', split_axis=0, concat_axis=2, tiled=True)  14.4 us
    dot_general x1, matrix products, shards(): jnp.dot(all_rows, w_both, preferred_element_type=jnp.float32)  11.3 us
    dot_general x1, matrix products, shards(): jnp.dot(lax.all_gather(hidden, 'seq', axis=0, tiled=True), down_weight, p...  7.26 us
  transfers between devices with their start and end apart: 3, of which 2 were waited for; matrix products, arithmetic and copies ran while one was open for 0% of the time, Pallas kernels for 0%

profile of v1, /device:TPU:1, one launch (start us, length us, event | category | flops | bytes accessed | tf_op | source)
XLA Modules:
  0.0 329.0 jit_solution(8701469700639723766)
XLA Ops:
  6.5 0.0 copy-start
  6.5 0.0 reduce-scatter.2.cloned.1.call-start
  6.5 1.1 slice.34
  7.6 4.9 %collective-permute-start = (bf16[3,8192]{1,0:T(4,128)(2,1)S(1)}, bf16[3,8192]{1,0:T(4,128)(2,1)S(1)}, u32[]{:S(2)}, u32[]{:S(2)}) collective-permute-start(bf16[3,8192]{1,0:T(4,128)(2,1)S(1)} %slice.34), channel_id=1, source_target_pairs={{0,8},{8,16},{16,24},{24,32},{32,40},{40,48},{48,56},{56,64},{64,7... | collective-permute-start | bytes 147464 | tf_op jit(solution)/shard_map/ppermute | solution.py:17
  12.5 1.3 fusion.25
  13.8 0.0 collective-permute-done
  13.9 2.2 maximum_convert_fusion
  16.1 0.0 copy-start.1
  16.1 2.2 multiply_reduce_fusion
  18.3 0.0 copy-done.1
  18.3 0.5 multiply_convert_fusion
  19.1 0.0 copy-start.2
  19.1 0.0 copy-start.3
  19.1 36.8 %all_to_all.25 = bf16[16,128,512]{2,1,0:T(8,128)(2,1)S(1)} all-to-all(bf16[16,128,512]{2,1,0:T(8,128)(2,1)S(1)} %fusion.7), channel_id=1, replica_groups=mesh['seq'=16,'tp'=8] {'seq'}, dimensions={0} | all-to-all | bytes 4194304 | tf_op jit(solution)/shard_map/all_to_all | solution.py:10
  56.0 0.0 copy-done.2
  56.0 0.0 copy-done.3
  56.0 11.3 %convolution_convert_fusion = bf16[2048,3584]{1,0:T(8,128)(2,1)} fusion(bf16[2048,512]{1,0:T(8,128)(2,1)S(1)} %bitcast.85, bf16[512,1792]{1,0:T(8,128)(2,1)S(1)} %copy-done.2, bf16[512,1792]{1,0:T(8,128)(2,1)S(1)} %copy-done.3), kind=kOutput, calls=%fused_computation | convolution fusion | flops 7530872832 | bytes 20447232 | tf_op jit(solution)/shard_map/dot_general | solution.py:52
  67.3 0.0 reduce-scatter.2.cloned.1.call-update
  67.3 0.0 all-gather.2.cloned.1.call-start
  67.4 129.9 %reduce-scatter.2.cloned.1.call-done = bf16[128,3584]{1,0:T(8,128)(2,1)} async-done(((bf16[2048,3584]{1,0:T(8,128)(2,1)}), bf16[128,3584]{1,0:T(8,128)(2,1)}) %reduce-scatter.2.cloned.1.call-update) | async-done | bytes 917520 | tf_op jit(solution)/shard_map/reduce_scatter | solution.py:51
  197.2 1.4 convert_element_type.27
  198.6 1.0 fusion.6
  199.6 0.0 all-gather.2.cloned.1.call-update
  199.7 67.8 %all-gather.2.cloned.1.call-done = bf16[2048,1792]{1,0:T(8,128)(2,1)} async-done(((bf16[128,1792]{1,0:T(8,128)(2,1)}), bf16[2048,1792]{1,0:T(8,128)(2,1)}) %all-gather.2.cloned.1.call-update) | async-done | bytes 7340048 | tf_op jit(solution)/shard_map/all_gather | solution.py:59
  267.5 0.0 copy-done
  267.5 7.3 %convolution_convert_fusion.1 = bf16[2048,512]{1,0:T(8,128)(2,1)S(1)} fusion(bf16[2048,1792]{1,0:T(8,128)(2,1)} %all-gather.2.cloned.1.call-done, bf16[1792,512]{1,0:T(8,128)(2,1)S(1)} %copy-done), kind=kOutput, calls=%fused_computation.13 | convolution fusion | flops 3759144960 | bytes 11272192 | tf_op jit(solution)/shard_map/dot_general | solution.py:58
  274.7 0.2 copy.16
  274.9 30.1 %all_to_all.26 = bf16[8,16,16,512]{3,2,1,0:T(8,128)(2,1)} all-to-all(bf16[8,16,16,512]{3,2,1,0:T(8,128)(2,1)S(1)} %bitcast.84), channel_id=1, replica_groups=mesh['seq'=16,'tp'=8] {'tp'}, dimensions={0} | all-to-all | bytes 4194304 | tf_op jit(solution)/shard_map/all_to_all | solution.py:28
  305.1 2.0 reduce_sum.22
  307.0 14.4 %all_to_all.27 = bf16[16,16,512]{2,1,0:T(8,128)(2,1)S(1)} all-to-all(bf16[16,16,512]{2,1,0:T(8,128)(2,1)S(1)} %reduce_sum.22), channel_id=1, replica_groups=mesh['seq'=16,'tp'=8] {'seq'}, dimensions={0} | all-to-all | bytes 524288 | tf_op jit(solution)/shard_map/all_to_all | solution.py:67
  321.4 0.7 copy.13
  (17 shorter events, 0.2 us)
Async XLA Ops:
  6.5 260.9 %copy-start = (bf16[1792,512]{1,0:T(8,128)(2,1)S(1)}, bf16[1792,512]{1,0:T(8,128)(2,1)}, u32[]{:S(2)}) copy-start(bf16[1792,512]{1,0:T(8,128)(2,1)} %param.11) | copy-start | bytes 5505028
  6.5 190.7 %reduce-scatter.2.cloned.1.call-start = ((), (), s32[]{:S(2)}) async-start(), calls=%async_computation.4 | async-start | bytes 15597568 | tf_op jit(solution)/shard_map/reduce_scatter | solution.py:51
  7.6 6.2 %collective-permute-start = (bf16[3,8192]{1,0:T(4,128)(2,1)S(1)}, bf16[3,8192]{1,0:T(4,128)(2,1)S(1)}, u32[]{:S(2)}, u32[]{:S(2)}) collective-permute-start(bf16[3,8192]{1,0:T(4,128)(2,1)S(1)} %slice.34), channel_id=1, source_target_pairs={{0,8},{8,16},{16,24},{24,32},{32,40},{40,48},{48,56},{56,64},{64,7... | collective-permute-start | bytes 147464 | tf_op jit(solution)/shard_map/ppermute | solution.py:17
  16.1 2.2 copy-start.1
  19.1 36.9 %copy-start.2 = (bf16[512,1792]{1,0:T(8,128)(2,1)S(1)}, bf16[512,1792]{1,0:T(8,128)(2,1)}, u32[]{:S(2)}) copy-start(bf16[512,1792]{1,0:T(8,128)(2,1)} %param.10) | copy-start | bytes 5505028
  19.1 36.9 %copy-start.3 = (bf16[512,1792]{1,0:T(8,128)(2,1)S(1)}, bf16[512,1792]{1,0:T(8,128)(2,1)}, u32[]{:S(2)}) copy-start(bf16[512,1792]{1,0:T(8,128)(2,1)} %param.9) | copy-start | bytes 5505028
  67.3 200.1 %all-gather.2.cloned.1.call-start = ((), (), s32[]{:S(2)}) async-start(), calls=%async_computation.5 | async-start | bytes 7798784 | tf_op jit(solution)/shard_map/all_gather | solution.py:59
Sparse Core Ops, SparseCore 0:
  67.5 129.7 reduce-scatter.1
  199.8 67.6 all-gather.1
